TPU v7x, 32 devices: a whole 2x2x4 slice. The times are simulated.
32 devices in a mesh: level: 4 (over z), dev: 8 (over y, x, core).
Axes of the slice: x: 2, y: 2, z: 4, core: 2. Of those that a mesh axis runs over, the one named last changes fastest.
Arguments:
- fields: float32 [4, 128, 12, 128], P('level', 'dev'), may hold values from -6 to 6
- own_src: int32 [4, 128], P('level', 'dev'), may hold values from 0 to 15
- own_weight: bfloat16 [4, 128, 128, 128], P('level', 'dev'), may hold values from 0 to 1, as said below
- send_block: int32 [4, 8, 8, 2], P('level', 'dev'), may hold values from 0 to 15
- send_target: int32 [4, 8, 8, 2], P('level', 'dev'), may hold values from 0 to 15
- send_count: int32 [4, 8, 8], P('level', 'dev'), may hold values from 0 to 2, as said below
- send_weight: bfloat16 [4, 8, 8, 2, 128, 128], P('level', 'dev'), may hold values from 0 to 1, as said below
- left_block: int32 [4, 8, 4, 2], P('level', 'dev'), may hold values from 0 to 15
- left_target: int32 [4, 8, 4, 2], P('level', 'dev'), may hold values from 0 to 15
- left_count: int32 [4, 8, 4], P('level', 'dev'), may hold values from 0 to 2, as said below
- left_weight: bfloat16 [4, 8, 4, 2, 128, 128], P('level', 'dev'), may hold values from 0 to 1, as said below
Outputs:
- remapped: float32 [4, 128, 12, 128], P('level', 'dev')
- totals: float32 [12], replicated
Inputs may be any that keep to these rules, and one draw needn't show every extreme that they name: send_count[l, s, s] = 0; for every level some receiver device gets 2 live slots from every other device of the level. left_count[m, q, m] = 0; for every device index some receiver level gets 2 live slots from every other level. `own_weight`: nonnegative; entry [k, i] is zero where old cell k and new cell i differ by more than 3; each column sums to a positive intersect fraction of at most 1. `send_weight`: nonnegative; entry [k, i] is zero where old cell k and new cell i differ by more than 3; each column sums to a positive intersect fraction of at most 1. `left_weight`: nonnegative; entry [k, i] is zero where old cell k and new cell i differ by more than 3; each column sums to a positive intersect fraction of at most 1.
All inputs are finite; a program needn't handle non-finite values.
Results may differ from a plain program's by a relative error of at most 0.0045.
Values may be sent and summed in bfloat16 or wider, within the bound.
A program may use at most 64 MiB of HBM per device.

v0:
```python
import functools

import jax
import jax.numpy as jnp
from jax import lax
from jax.experimental import pallas as pl
from jax.experimental.pallas import tpu as pltpu
from jax.sharding import PartitionSpec as P

MESH = pl.DeviceIdType.MESH
F32 = jnp.float32
BF16 = jnp.bfloat16


def kernel(
    nd,
    nl,
    direct,
    own_src_hbm,
    send_block_hbm,
    send_target_hbm,
    send_count_hbm,
    left_block_hbm,
    left_target_hbm,
    left_count_hbm,
    fields_hbm,
    own_hbm,
    send_hbm,
    left_hbm,
    out_ref,
    tot_ref,
    own_src,
    send_block,
    send_target,
    send_count,
    left_block,
    left_target,
    left_count,
    fields,
    own_w,
    send_w,
    left_w,
    load_sem,
    sbuf,
    rbuf,
    s_sem,
    r_sem,
    lsbuf,
    lrbuf,
    ls_sem,
    lr_sem,
    tbuf,
    trecv,
    ts_sem,
    tr_sem,
    ubuf,
    urecv,
    us_sem,
    ur_sem,
):
    dev = lax.axis_index("dev")
    lvl = lax.axis_index("level")
    blocks, cells = own_w.shape[:2]
    comp = fields.shape[0] // blocks
    cap = send_w.shape[1]
    lcap = left_w.shape[1]
    rows = sbuf.shape[1] // cap

    barrier = pltpu.get_barrier_semaphore()
    left_peers = [lax.rem(lvl + r, nl) for r in range(1, nl)]
    send_peers = [lax.rem(dev + r, nd) for r in range(1, nd)]
    pairs = (
        (left_block_hbm, left_block),
        (left_target_hbm, left_target),
        (left_count_hbm, left_count),
        (fields_hbm, fields),
        *[(left_hbm.at[p], left_w.at[p]) for p in left_peers],
        (send_block_hbm, send_block),
        (send_target_hbm, send_target),
        (send_count_hbm, send_count),
        *[(send_hbm.at[p], send_w.at[p]) for p in send_peers],
        (own_src_hbm, own_src),
        (own_hbm, own_w),
    )
    loads = [
        pltpu.make_async_copy(src, dst, load_sem.at[i]) for i, (src, dst) in enumerate(pairs)
    ]
    for load in loads:
        load.start()

    def peer_of(l, r):
        return {"level": lax.rem(lvl + l, nl), "dev": lax.rem(dev + r, nd)}

    offsets = [
        (l, r)
        for l in reversed(range(nl))
        for r in reversed(range(nd))
        if (l or r) and (direct or not (l and r))
    ]
    for l, r in offsets:
        pl.semaphore_signal(barrier, inc=1, device_id=peer_of(l, r), device_id_type=MESH)

    part = jnp.zeros((comp, cells), F32)

    def donor(index):
        return fields[pl.ds(index, comp, stride=blocks), :]

    def product(block, weight):
        return jnp.dot(block.astype(BF16), weight, preferred_element_type=F32)

    def message(buf, r, c, slot_block, slot_target, slot_count, weights, peer):
        block = donor(slot_block[c, peer])
        block = jnp.where(c < slot_count[0, peer], block, jnp.zeros_like(block))
        term = product(block, weights[peer, c])
        target = jnp.full((rows - comp, cells), slot_target[c, peer].astype(F32), F32)
        buf[r, c * rows : (c + 1) * rows, :] = jnp.concatenate([term, target], axis=0).astype(BF16)
        return term

    first = 4 + len(left_peers)
    second = first + 3 + len(send_peers)
    for load in loads[:first]:
        load.wait()
    for r in range(1, nl):
        peer = lax.rem(lvl + r, nl)
        for c in range(lcap):
            part += message(lsbuf, r, c, left_block, left_target, left_count, left_w, peer)
    for load in loads[first:second]:
        load.wait()
    for r in range(1, nd):
        peer = lax.rem(dev + r, nd)
        for c in range(cap):
            part += message(sbuf, r, c, send_block, send_target, send_count, send_w, peer)

    for load in loads[second:]:
        load.wait()
    acc = []
    for b in range(blocks):
        term = product(donor(own_src[0, b]), own_w[b])
        part += term
        acc.append(term)

    sums = jnp.sum(part, axis=1, keepdims=True)
    same = lax.broadcasted_iota(jnp.int32, (comp, cells), 0) == lax.broadcasted_iota(
        jnp.int32, (comp, cells), 1
    )
    row = jnp.sum(jnp.where(same, sums, 0.0), axis=0, keepdims=True)
    tbuf[...] = row

    pl.semaphore_wait(barrier, len(offsets))

    sends = []

    def send(src, dst, s, d, who):
        copy = pltpu.make_async_remote_copy(
            src_ref=src, dst_ref=dst, send_sem=s, recv_sem=d, device_id=who, device_id_type=MESH
        )
        copy.start()
        sends.append(copy)
        return copy

    if direct:
        tops = [
            send(tbuf, urecv.at[i], us_sem.at[i], ur_sem.at[i], peer_of(l, r))
            for i, (l, r) in enumerate(offsets)
        ]
    else:
        tots = [
            send(tbuf, trecv.at[r], ts_sem.at[r], tr_sem.at[r], peer_of(0, r))
            for r in range(1, nd)
        ]
    lefts = [
        send(lsbuf.at[r], lrbuf.at[r], ls_sem.at[r], lr_sem.at[r], peer_of(r, 0))
        for r in range(1, nl)
    ]
    intras = [
        send(sbuf.at[r], rbuf.at[r], s_sem.at[r], r_sem.at[r], peer_of(0, r)) for r in range(1, nd)
    ]
    if not direct:
        for r, copy in enumerate(tots, 1):
            copy.wait_recv()
            row += trecv[r]
        ubuf[...] = row
        tops = [
            send(ubuf, urecv.at[i], us_sem.at[i], ur_sem.at[i], peer_of(i + 1, 0))
            for i in range(nl - 1)
        ]

    def place(buf, r, slots):
        for c in range(slots):
            got = buf[r, c * rows : (c + 1) * rows, :].astype(F32)
            term = got[:comp]
            target = jnp.broadcast_to(got[comp : comp + 1], (comp, cells))
            for b in range(blocks):
                acc[b] = acc[b] + jnp.where(target == float(b), term, 0.0)

    for r, copy in enumerate(intras, 1):
        copy.wait_recv()
        place(rbuf, r, cap)
    for r, copy in enumerate(lefts, 1):
        copy.wait_recv()
        place(lrbuf, r, lcap)
    for b in range(blocks):
        out_ref[pl.ds(b, comp, stride=blocks), :] = acc[b]
    for copy in sends:
        copy.wait_send()
    for copy in tops:
        copy.wait_recv()
    terms = [row] + [urecv[i] for i in range(len(tops))]
    while len(terms) > 1:
        half = len(terms) // 2
        terms = [a + b for a, b in zip(terms[:half], terms[half:])] + terms[2 * half :]
    row = terms[0]
    tot_ref[...] = (row / (cells * blocks))[0, :comp]


def solution(mesh):
    nd = mesh.shape["dev"]
    nl = mesh.shape["level"]
    direct = nd * nl <= 64
    last = (nd if direct else 1) * nl

    def body(
        fields,
        own_src,
        own_weight,
        send_block,
        send_target,
        send_count,
        send_weight,
        left_block,
        left_target,
        left_count,
        left_weight,
    ):
        blocks, comp, cells = fields.shape[1:]
        cap = send_weight.shape[3]
        lcap = left_weight.shape[3]
        rows = -(-(comp + 1) // 16) * 16
        smem = functools.partial(pltpu.SMEM, dtype=jnp.int32)
        hbm = pl.BlockSpec(memory_space=pl.ANY)
        vmem = pl.BlockSpec(memory_space=pltpu.VMEM)
        dma = pltpu.SemaphoreType.DMA
        remapped, totals = pl.pallas_call(
            functools.partial(kernel, nd, nl, direct),
            out_shape=(
                pltpu.VMEM((comp * blocks, cells), F32),
                pltpu.VMEM((comp,), F32),
            ),
            in_specs=[hbm] * 11,
            out_specs=(vmem, vmem),
            scratch_shapes=[
                smem((1, blocks)),
                smem((cap, nd)),
                smem((cap, nd)),
                smem((1, nd)),
                smem((lcap, nl)),
                smem((lcap, nl)),
                smem((1, nl)),
                pltpu.VMEM((comp * blocks, cells), F32),
                pltpu.VMEM((blocks, cells, cells), BF16),
                pltpu.VMEM((nd, cap, cells, cells), BF16),
                pltpu.VMEM((nl, lcap, cells, cells), BF16),
                dma((9 + nd + nl,)),
                pltpu.VMEM((nd, cap * rows, cells), BF16),
                pltpu.VMEM((nd, cap * rows, cells), BF16),
                dma((nd,)),
                dma((nd,)),
                pltpu.VMEM((nl, lcap * rows, cells), BF16),
                pltpu.VMEM((nl, lcap * rows, cells), BF16),
                dma((nl,)),
                dma((nl,)),
                pltpu.VMEM((1, cells), F32),
                pltpu.VMEM((nd, 1, cells), F32),
                dma((nd,)),
                dma((nd,)),
                pltpu.VMEM((1, cells), F32),
                pltpu.VMEM((last, 1, cells), F32),
                dma((last,)),
                dma((last,)),
            ],
            compiler_params=pltpu.CompilerParams(collective_id=0, has_side_effects=True),
        )(
            own_src,
            send_block[0, 0].T,
            send_target[0, 0].T,
            send_count[0],
            left_block[0, 0].T,
            left_target[0, 0].T,
            left_count[0],
            fields[0].transpose(1, 0, 2).reshape(comp * blocks, cells),
            own_weight[0],
            send_weight[0, 0],
            left_weight[0, 0],
        )
        remapped = remapped.reshape(comp, blocks, cells).transpose(1, 0, 2)
        return remapped[None], totals

    in_specs = (
        P("level", "dev", None, None),
        P("level", "dev"),
        P("level", "dev", None, None),
        P("level", "dev", None, None),
        P("level", "dev", None, None),
        P("level", "dev", None),
        P("level", "dev", None, None, None, None),
        P("level", "dev", None, None),
        P("level", "dev", None, None),
        P("level", "dev", None),
        P("level", "dev", None, None, None, None),
    )
    out_specs = (P("level", "dev", None, None), P())
    return jax.shard_map(body, mesh=mesh, in_specs=in_specs, out_specs=out_specs, check_vma=False)
```

profile of v0, /device:TPU:0, one launch (start us, length us, event | category | flops | bytes accessed | tf_op | source)
XLA Modules:
  0.0 13.3 jit_solution(9197234395047676893)
XLA Ops:
  0.6 11.5 %shard_map.122 = (f32[192,128]{1,0:T(8,128)S(1)}, f32[12]{0:T(128)S(1)}) custom-call(s32[1,16]{1,0:T(1,128)} %own_src_hbm.1, s32[2,8]{1,0:T(2,128)} %bitcast.32, s32[2,8]{1,0:T(2,128)} %bitcast.33, s32[1,8]{1,0:T(1,128)} %bitcast.36, s32[2,4]{1,0:T(2,128)} %bitcast.34, s32[2,4]{1,0:T(2,128)} %bitcast.35, s32[1,4]{1,0:T(1,128)} %bitcast.37, ...), custom_call_target="tpu_custom_call" | custom-call | tf_op jit(solution)/shard_map/pallas_call | solution.py:243
  12.2 0.6 %copy.15 = f32[1,16,12,128]{3,1,2,0:T(8,128)} copy(f32[1,16,12,128]{3,1,2,0:T(8,128)S(1)} %bitcast.27) | data formatting | bytes 196608
  12.8 0.5 %copy.16 = f32[12]{0:T(128)} copy(f32[12]{0:T(128)S(1)} %get-tuple-element.7) | data formatting | bytes 96
where the time goes:
time: 13.5 us; the launch traced here: 13.3 us
  Pallas kernels  11.5 us (85%)
  local copies, waits for them, and re-layouts  1.15 us (9%)
  between operations  0.64 us (5%)
    pallas_call x1, Pallas kernels, body(): pl.pallas_call(functools.partial(kernel, nd, nl, direct), out_shape=(pltp...  11.5 us
    unnamed x2, local copies, waits for them, and re-layouts  1.15 us

commit v1 on v0

v1 whole, which is shorter than its diff:
```python
import functools

import jax
import jax.numpy as jnp
from jax import lax
from jax.experimental import pallas as pl
from jax.experimental.pallas import tpu as pltpu
from jax.sharding import PartitionSpec as P

MESH = pl.DeviceIdType.MESH
F32 = jnp.float32
BF16 = jnp.bfloat16
CHUNKS = 4


def kernel(
    nd,
    nl,
    direct,
    own_src_hbm,
    send_block_hbm,
    send_target_hbm,
    send_count_hbm,
    left_block_hbm,
    left_target_hbm,
    left_count_hbm,
    fields_hbm,
    own_hbm,
    send_hbm,
    left_hbm,
    out_ref,
    tot_ref,
    own_src,
    send_block,
    send_target,
    send_count,
    left_block,
    left_target,
    left_count,
    fields,
    own_w,
    send_w,
    left_w,
    load_sem,
    sbuf,
    rbuf,
    lsbuf,
    lrbuf,
    tbuf,
    trecv,
    urecv,
    move_sem,
):
    dev = lax.axis_index("dev")
    lvl = lax.axis_index("level")
    blocks, cells = own_w.shape[:2]
    comp = fields.shape[0] // blocks
    cap = send_w.shape[1]
    lcap = left_w.shape[1]
    rows = sbuf.shape[1] // cap
    per = blocks // CHUNKS

    barrier = pltpu.get_barrier_semaphore()
    left_peers = [lax.rem(lvl + r, nl) for r in range(1, nl)]
    send_peers = [lax.rem(dev + r, nd) for r in range(1, nd)]

    def load(src, dst, i):
        copy = pltpu.make_async_copy(src, dst, load_sem.at[i])
        copy.start()
        return copy

    small = [
        load(src, dst, i)
        for i, (src, dst) in enumerate(
            (
                (left_block_hbm, left_block),
                (left_target_hbm, left_target),
                (left_count_hbm, left_count),
                (send_block_hbm, send_block),
                (send_target_hbm, send_target),
                (send_count_hbm, send_count),
                (own_src_hbm, own_src),
                (fields_hbm, fields),
            )
        )
    ]
    n = len(small)
    for i, p in enumerate(left_peers):
        load(left_hbm.at[p], left_w.at[i], n)
    for i, p in enumerate(send_peers):
        load(send_hbm.at[p], send_w.at[i], n + 1)
    owns = [
        load(own_hbm.at[i * per : (i + 1) * per], own_w.at[i * per : (i + 1) * per], n + 2 + i)
        for i in range(CHUNKS)
    ]

    def peer_of(l, r):
        return {"level": lax.rem(lvl + l, nl), "dev": lax.rem(dev + r, nd)}

    offsets = [
        (l, r)
        for l in range(nl)
        for r in range(nd)
        if (l or r) and (direct or not (l and r))
    ]
    for l, r in offsets:
        pl.semaphore_signal(barrier, inc=1, device_id=peer_of(l, r), device_id_type=MESH)

    part = jnp.zeros((comp, cells), F32)

    def donor(index):
        return fields[pl.ds(index, comp, stride=blocks), :]

    def product(block, weight):
        return jnp.dot(block.astype(BF16), weight, preferred_element_type=F32)

    def message(buf, i, c, slot_block, slot_target, slot_count, weights, peer):
        block = donor(slot_block[c, peer])
        block = jnp.where(c < slot_count[0, peer], block, jnp.zeros_like(block))
        term = product(block, weights[i, c])
        target = jnp.full((rows - comp, cells), slot_target[c, peer].astype(F32), F32)
        buf[i, c * rows : (c + 1) * rows, :] = jnp.concatenate([term, target], axis=0).astype(BF16)
        return term

    def settle(ref, sem):
        pltpu.make_async_copy(ref, ref, sem).wait()

    for copy in small:
        copy.wait()
    settle(left_w, load_sem.at[n])
    for i, peer in enumerate(left_peers):
        for c in range(lcap):
            part += message(lsbuf, i, c, left_block, left_target, left_count, left_w, peer)
    settle(send_w, load_sem.at[n + 1])
    for i, peer in enumerate(send_peers):
        for c in range(cap):
            part += message(sbuf, i, c, send_block, send_target, send_count, send_w, peer)
    acc = []
    for b in range(blocks):
        if b % per == 0:
            owns[b // per].wait()
        term = product(donor(own_src[0, b]), own_w[b])
        part += term
        acc.append(term)

    sums = jnp.sum(part, axis=1, keepdims=True)
    same = lax.broadcasted_iota(jnp.int32, (comp, cells), 0) == lax.broadcasted_iota(
        jnp.int32, (comp, cells), 1
    )
    row = jnp.sum(jnp.where(same, sums, 0.0), axis=0, keepdims=True)
    tbuf[0] = row

    pl.semaphore_wait(barrier, len(offsets))

    def send(src, dst, s, who):
        pltpu.make_async_remote_copy(
            src_ref=src,
            dst_ref=dst,
            send_sem=move_sem.at[2 * s],
            recv_sem=move_sem.at[2 * s + 1],
            device_id=who,
            device_id_type=MESH,
        ).start()

    if direct:
        for i, (l, r) in enumerate(offsets):
            send(tbuf.at[0], urecv.at[i], 0, peer_of(l, r))
    else:
        for r in range(1, nd):
            send(tbuf.at[0], trecv.at[r - 1], 3, peer_of(0, r))
    for r in range(1, nl):
        send(lsbuf.at[r - 1], lrbuf.at[r - 1], 1, peer_of(r, 0))
    for r in range(1, nd):
        send(sbuf.at[r - 1], rbuf.at[r - 1], 2, peer_of(0, r))
    if not direct:
        settle(trecv, move_sem.at[7])
        row = row + jnp.sum(trecv[...], axis=0)
        tbuf[1] = row
        for r in range(1, nl):
            send(tbuf.at[1], urecv.at[r - 1], 0, peer_of(r, 0))

    def place(buf, i, slots):
        for c in range(slots):
            got = buf[i, c * rows : (c + 1) * rows, :].astype(F32)
            term = got[:comp]
            target = jnp.broadcast_to(got[comp : comp + 1], (comp, cells))
            for b in range(blocks):
                acc[b] = acc[b] + jnp.where(target == float(b), term, 0.0)

    settle(rbuf, move_sem.at[5])
    for i in range(nd - 1):
        place(rbuf, i, cap)
    settle(lrbuf, move_sem.at[3])
    for i in range(nl - 1):
        place(lrbuf, i, lcap)
    for b in range(blocks):
        out_ref[pl.ds(b, comp, stride=blocks), :] = acc[b]
    settle(sbuf, move_sem.at[4])
    settle(lsbuf, move_sem.at[2])
    settle(urecv, move_sem.at[0])
    if not direct:
        settle(trecv, move_sem.at[6])
    settle(urecv, move_sem.at[1])
    terms = [row] + [urecv[i] for i in range(urecv.shape[0])]
    while len(terms) > 1:
        half = len(terms) // 2
        terms = [a + b for a, b in zip(terms[:half], terms[half:])] + terms[2 * half :]
    tot_ref[...] = (terms[0] / (cells * blocks))[0, :comp]


def finish(remapped_vmem, totals_vmem, remapped_hbm, totals_hbm, sem):
    copies = [
        pltpu.make_async_copy(remapped_vmem, remapped_hbm, sem.at[0]),
        pltpu.make_async_copy(totals_vmem, totals_hbm, sem.at[1]),
    ]
    for copy in copies:
        copy.start()
    for copy in copies:
        copy.wait()


def solution(mesh):
    nd = mesh.shape["dev"]
    nl = mesh.shape["level"]
    direct = nd * nl <= 64
    last = (nd * nl if direct else nl) - 1

    def body(
        fields,
        own_src,
        own_weight,
        send_block,
        send_target,
        send_count,
        send_weight,
        left_block,
        left_target,
        left_count,
        left_weight,
    ):
        blocks, comp, cells = fields.shape[1:]
        cap = send_weight.shape[3]
        lcap = left_weight.shape[3]
        rows = -(-(comp + 1) // 16) * 16
        smem = functools.partial(pltpu.SMEM, dtype=jnp.int32)
        hbm = pl.BlockSpec(memory_space=pl.ANY)
        vmem = pl.BlockSpec(memory_space=pltpu.VMEM)
        dma = pltpu.SemaphoreType.DMA
        remapped, totals = pl.pallas_call(
            functools.partial(kernel, nd, nl, direct),
            out_shape=(
                pltpu.VMEM((comp * blocks, cells), F32),
                pltpu.VMEM((comp,), F32),
            ),
            in_specs=[hbm] * 11,
            out_specs=(vmem, vmem),
            scratch_shapes=[
                smem((1, blocks)),
                smem((cap, nd)),
                smem((cap, nd)),
                smem((1, nd)),
                smem((lcap, nl)),
                smem((lcap, nl)),
                smem((1, nl)),
                pltpu.VMEM((comp * blocks, cells), F32),
                pltpu.VMEM((blocks, cells, cells), BF16),
                pltpu.VMEM((nd - 1, cap, cells, cells), BF16),
                pltpu.VMEM((nl - 1, lcap, cells, cells), BF16),
                dma((10 + CHUNKS,)),
                pltpu.VMEM((nd - 1, cap * rows, cells), BF16),
                pltpu.VMEM((nd - 1, cap * rows, cells), BF16),
                pltpu.VMEM((nl - 1, lcap * rows, cells), BF16),
                pltpu.VMEM((nl - 1, lcap * rows, cells), BF16),
                pltpu.VMEM((2, 1, cells), F32),
                pltpu.VMEM((nd - 1, 1, cells), F32),
                pltpu.VMEM((last, 1, cells), F32),
                dma((6 if direct else 8,)),
            ],
            compiler_params=pltpu.CompilerParams(collective_id=0, has_side_effects=True),
        )(
            own_src,
            send_block[0, 0].T,
            send_target[0, 0].T,
            send_count[0],
            left_block[0, 0].T,
            left_target[0, 0].T,
            left_count[0],
            fields[0].transpose(1, 0, 2).reshape(comp * blocks, cells),
            own_weight[0],
            send_weight[0, 0],
            left_weight[0, 0],
        )
        remapped, totals = pl.pallas_call(
            finish,
            out_shape=(
                jax.ShapeDtypeStruct((comp * blocks, cells), F32),
                jax.ShapeDtypeStruct((comp,), F32),
            ),
            in_specs=[vmem, vmem],
            out_specs=(hbm, hbm),
            scratch_shapes=[dma((2,))],
        )(
            pltpu.with_memory_space_constraint(remapped, pltpu.VMEM),
            pltpu.with_memory_space_constraint(totals, pltpu.VMEM),
        )
        remapped = remapped.reshape(comp, blocks, cells).transpose(1, 0, 2)
        return remapped[None], totals

    in_specs = (
        P("level", "dev", None, None),
        P("level", "dev"),
        P("level", "dev", None, None),
        P("level", "dev", None, None),
        P("level", "dev", None, None),
        P("level", "dev", None),
        P("level", "dev", None, None, None, None),
        P("level", "dev", None, None),
        P("level", "dev", None, None),
        P("level", "dev", None),
        P("level", "dev", None, None, None, None),
    )
    out_specs = (P("level", "dev", None, None), P())
    return jax.shard_map(body, mesh=mesh, in_specs=in_specs, out_specs=out_specs, check_vma=False)
```

time: 13.5 us -> 12.3 us (0.911)
  local copies, waits for them, and re-layouts: 1.15 us -> 0 us
    unnamed x2 -> x0, local copies, waits for them, and re-layouts: 1.15 us -> none
    pallas_call x1, Pallas kernels: 11.5 us -> 10.8 us  [body(): pl.pallas_call(functools.partial(kernel, nd, nl, direct), out_shape=(pltp...]
    pallas_call x0 -> x1, Pallas kernels: none -> 0.66 us  [body(): pl.pallas_call(finish, out_shape=(jax.ShapeDtypeStruct((comp * blocks, ce...]
where the time goes in v1:
time: 12.3 us; the launch traced here: 12.1 us
  Pallas kernels  11.5 us (93%)
  between operations  0.64 us (5%)
    pallas_call x1, Pallas kernels, body(): pl.pallas_call(functools.partial(kernel, nd, nl, direct), out_shape=(pltp...  10.8 us
    pallas_call x1, Pallas kernels, body(): pl.pallas_call(finish, out_shape=(jax.ShapeDtypeStruct((comp * blocks, ce...  0.66 us

profile of v1, /device:TPU:0, one launch (start us, length us, event | category | flops | bytes accessed | tf_op | source)
XLA Modules:
  0.0 12.1 jit_solution(11623823398491428409)
XLA Ops:
  0.6 10.8 %shard_map.122 = (f32[192,128]{1,0:T(8,128)S(1)}, f32[12]{0:T(128)S(1)}) custom-call(s32[1,16]{1,0:T(1,128)} %own_src_hbm.1, s32[2,8]{1,0:T(2,128)} %bitcast.31, s32[2,8]{1,0:T(2,128)} %bitcast.32, s32[1,8]{1,0:T(1,128)} %bitcast.35, s32[2,4]{1,0:T(2,128)} %bitcast.33, s32[2,4]{1,0:T(2,128)} %bitcast.34, s32[1,4]{1,0:T(1,128)} %bitcast.36, ...), custom_call_target="tpu_custom_call" | custom-call | tf_op jit(solution)/shard_map/pallas_call | solution.py:249
  11.4 0.7 %shard_map.123 = (f32[192,128]{1,0:T(8,128)}, f32[12]{0:T(128)}) custom-call(f32[192,128]{1,0:T(8,128)S(1)} %get-tuple-element.6.remapped_vmem, f32[12]{0:T(128)S(1)} %get-tuple-element.7.totals_vmem), custom_call_target="tpu_custom_call" | custom-call | tf_op jit(solution)/shard_map/pallas_call | solution.py:293

commit v2 on v1

v2 whole, which is shorter than its diff:
```python
import functools

import jax
import jax.numpy as jnp
from jax import lax
from jax.experimental import pallas as pl
from jax.experimental.pallas import tpu as pltpu
from jax.sharding import PartitionSpec as P

MESH = pl.DeviceIdType.MESH
F32 = jnp.float32
BF16 = jnp.bfloat16
CHUNKS = 1


def tree(terms):
    while len(terms) > 1:
        half = len(terms) // 2
        terms = [a + b for a, b in zip(terms[:half], terms[half:])] + terms[2 * half :]
    return terms[0]


def kernel(
    nd,
    nl,
    direct,
    own_src_hbm,
    send_block_hbm,
    send_target_hbm,
    send_count_hbm,
    left_block_hbm,
    left_target_hbm,
    left_count_hbm,
    fields_hbm,
    own_hbm,
    send_hbm,
    left_hbm,
    out_ref,
    tot_ref,
    own_src,
    send_block,
    send_target,
    send_count,
    left_block,
    left_target,
    left_count,
    fields,
    donors,
    own_w,
    send_w,
    left_w,
    sbuf,
    rbuf,
    lsbuf,
    lrbuf,
    tbuf,
    trecv,
    urecv,
    recv_sem,
):
    dev = lax.axis_index("dev")
    lvl = lax.axis_index("level")
    blocks, rows, cells = donors.shape
    comp = fields.shape[0] // blocks
    cap = send_w.shape[1]
    lcap = left_w.shape[1]
    per = blocks // CHUNKS

    barrier = pltpu.get_barrier_semaphore()
    left_peers = [lax.rem(lvl + r, nl) for r in range(1, nl)]
    send_peers = [lax.rem(dev + r, nd) for r in range(1, nd)]

    def settle(ref, sem):
        pltpu.make_async_copy(ref, ref, sem).wait()

    def peer_of(l, r):
        return {"level": lax.rem(lvl + l, nl), "dev": lax.rem(dev + r, nd)}

    offsets = [
        (l, r)
        for l in (*range(1, nl), 0)
        for r in (1, 2, 0, *range(3, nd))
        if (l or r) and (direct or not (l and r))
    ]

    def run(load_sem, send_sem):
        def load(src, dst, i):
            copy = pltpu.make_async_copy(src, dst, load_sem.at[i])
            copy.start()
            return copy

        small = [
            load(src, dst, i)
            for i, (src, dst) in enumerate(
                (
                    (fields_hbm, fields),
                    (left_block_hbm, left_block),
                    (left_target_hbm, left_target),
                    (left_count_hbm, left_count),
                    (send_block_hbm, send_block),
                    (send_target_hbm, send_target),
                    (send_count_hbm, send_count),
                    (own_src_hbm, own_src),
                )
            )
        ]
        n = len(small)
        owns = [
            load(own_hbm.at[i * per : (i + 1) * per], own_w.at[i * per : (i + 1) * per], n + 2 + i)
            for i in range(CHUNKS)
        ]

        for i, p in enumerate(send_peers):
            load(send_hbm.at[p], send_w.at[i], n + 1)
        for i, p in enumerate(left_peers):
            load(left_hbm.at[p], left_w.at[i], n)

        for l, r in offsets:
            pl.semaphore_signal(barrier, inc=1, device_id=peer_of(l, r), device_id_type=MESH)

        def products(pairs):
            terms = []
            for i in range(0, len(pairs), 2):
                group = pairs[i : i + 2]
                left = jnp.concatenate([block for block, _ in group], axis=0)
                right = jnp.concatenate([weight for _, weight in group], axis=1)
                both = jnp.dot(left, right, preferred_element_type=F32)
                for j in range(len(group)):
                    terms.append(both[j * rows : (j + 1) * rows, j * cells : (j + 1) * cells])
            return terms

        line = lax.broadcasted_iota(jnp.int32, (rows, cells), 0)

        held = []

        def messages(buf, slots, slot_block, slot_target, slot_count, weights, peers):
            keys = [(i, c, p) for i, p in enumerate(peers) for c in range(slots)]
            pairs = []
            for i, c, p in keys:
                block = donors[slot_block[c, p]]
                block = jnp.where(c < slot_count[0, p], block, jnp.zeros_like(block))
                pairs.append((block, weights[i, c]))
            terms = products(pairs)
            held.append((buf, slot_target, keys, terms))
            return terms

        def fill():
            for buf, slot_target, keys, terms in held:
                for (i, c, p), term in zip(keys, terms):
                    filled = jnp.where(line < comp, term, slot_target[c, p].astype(F32))
                    buf[i, c * rows : (c + 1) * rows, :] = filled.astype(BF16)

        small[0].wait()
        for b in range(blocks):
            block = fields[pl.ds(b, comp, stride=blocks), :]
            block = jnp.concatenate([block, jnp.zeros((rows - comp, cells), F32)], axis=0)
            donors[b] = block.astype(BF16)
        for copy in small[1:]:
            copy.wait()
        sent = []
        acc = []
        for i in range(CHUNKS):
            owns[i].wait()
            acc += products([(donors[own_src[0, b]], own_w[b]) for b in range(i * per, (i + 1) * per)])

        settle(send_w, load_sem.at[n + 1])
        settle(left_w, load_sem.at[n])
        sent += messages(sbuf, cap, send_block, send_target, send_count, send_w, send_peers)
        sent += messages(lsbuf, lcap, left_block, left_target, left_count, left_w, left_peers)
        part = tree(sent + acc)
        sums = jnp.sum(part, axis=1, keepdims=True)
        same = line == lax.broadcasted_iota(jnp.int32, (rows, cells), 1)
        row = jnp.sum(jnp.where(same, sums, 0.0), axis=0, keepdims=True)
        tbuf[0] = row

        pl.semaphore_wait(barrier, len(offsets))

        def send(src, dst, s, who):
            pltpu.make_async_remote_copy(
                src_ref=src,
                dst_ref=dst,
                send_sem=send_sem.at[s],
                recv_sem=recv_sem.at[s],
                device_id=who,
                device_id_type=MESH,
            ).start()

        if direct:
            for i, (l, r) in enumerate(offsets):
                send(tbuf.at[0], urecv.at[i], 0, peer_of(l, r))
        else:
            for r in range(1, nd):
                send(tbuf.at[0], trecv.at[r - 1], 3, peer_of(0, r))
        fill()
        for r in range(1, nl):
            send(lsbuf.at[r - 1], lrbuf.at[r - 1], 1, peer_of(r, 0))
        for r in range(1, nd):
            send(sbuf.at[r - 1], rbuf.at[r - 1], 2, peer_of(0, r))
        if not direct:
            settle(trecv, recv_sem.at[3])
            row = row + jnp.sum(trecv[...], axis=0)
            tbuf[1] = row
            for r in range(1, nl):
                send(tbuf.at[1], urecv.at[r - 1], 0, peer_of(r, 0))

        acc = [term[:comp] for term in acc]

        def place(buf, i, slots):
            for c in range(slots):
                got = buf[i, c * rows : (c + 1) * rows, :].astype(F32)
                term = got[:comp]
                target = jnp.broadcast_to(got[comp : comp + 1], (comp, cells))
                for b in range(blocks):
                    acc[b] = acc[b] + jnp.where(target == float(b), term, 0.0)

        settle(rbuf, recv_sem.at[2])
        for i in range(nd - 1):
            place(rbuf, i, cap)
        settle(lrbuf, recv_sem.at[1])
        for i in range(nl - 1):
            place(lrbuf, i, lcap)
        for b in range(blocks):
            out_ref[pl.ds(b, comp, stride=blocks), :] = acc[b]
        settle(sbuf, send_sem.at[2])
        settle(lsbuf, send_sem.at[1])
        settle(urecv, send_sem.at[0])
        if not direct:
            settle(trecv, send_sem.at[3])

    pl.run_scoped(
        run, pltpu.SemaphoreType.DMA((10 + CHUNKS,)), pltpu.SemaphoreType.DMA((recv_sem.shape[0],))
    )
    settle(urecv, recv_sem.at[0])
    mine = tbuf[0 if direct else 1]
    total = tree([mine] + [urecv[i] for i in range(urecv.shape[0])])
    tot_ref[...] = (total / (cells * blocks))[0, :comp]


def finish(remapped_vmem, totals_vmem, remapped_hbm, totals_hbm):
    def run(sem):
        copies = [
            pltpu.make_async_copy(remapped_vmem, remapped_hbm, sem.at[0]),
            pltpu.make_async_copy(totals_vmem, totals_hbm, sem.at[1]),
        ]
        for copy in copies:
            copy.start()
        for copy in copies:
            copy.wait()

    pl.run_scoped(run, pltpu.SemaphoreType.DMA((2,)))


def solution(mesh):
    nd = mesh.shape["dev"]
    nl = mesh.shape["level"]
    direct = nd * nl <= 64
    last = (nd * nl if direct else nl) - 1

    def body(
        fields,
        own_src,
        own_weight,
        send_block,
        send_target,
        send_count,
        send_weight,
        left_block,
        left_target,
        left_count,
        left_weight,
    ):
        blocks, comp, cells = fields.shape[1:]
        cap = send_weight.shape[3]
        lcap = left_weight.shape[3]
        rows = -(-(comp + 1) // 16) * 16
        smem = functools.partial(pltpu.SMEM, dtype=jnp.int32)
        hbm = pl.BlockSpec(memory_space=pl.ANY)
        vmem = pl.BlockSpec(memory_space=pltpu.VMEM)
        dma = pltpu.SemaphoreType.DMA
        remapped, totals = pl.pallas_call(
            functools.partial(kernel, nd, nl, direct),
            out_shape=(
                pltpu.VMEM((comp * blocks, cells), F32),
                pltpu.VMEM((comp,), F32),
            ),
            in_specs=[hbm] * 11,
            out_specs=(vmem, vmem),
            scratch_shapes=[
                smem((1, blocks)),
                smem((cap, nd)),
                smem((cap, nd)),
                smem((1, nd)),
                smem((lcap, nl)),
                smem((lcap, nl)),
                smem((1, nl)),
                pltpu.VMEM((comp * blocks, cells), F32),
                pltpu.VMEM((blocks, rows, cells), BF16),
                pltpu.VMEM((blocks, cells, cells), BF16),
                pltpu.VMEM((nd - 1, cap, cells, cells), BF16),
                pltpu.VMEM((nl - 1, lcap, cells, cells), BF16),
                pltpu.VMEM((nd - 1, cap * rows, cells), BF16),
                pltpu.VMEM((nd - 1, cap * rows, cells), BF16),
                pltpu.VMEM((nl - 1, lcap * rows, cells), BF16),
                pltpu.VMEM((nl - 1, lcap * rows, cells), BF16),
                pltpu.VMEM((2, 1, cells), F32),
                pltpu.VMEM((nd - 1, 1, cells), F32),
                pltpu.VMEM((last, 1, cells), F32),
                dma((3 if direct else 4,)),
            ],
            compiler_params=pltpu.CompilerParams(collective_id=0, has_side_effects=True),
        )(
            own_src,
            send_block[0, 0].T,
            send_target[0, 0].T,
            send_count[0],
            left_block[0, 0].T,
            left_target[0, 0].T,
            left_count[0],
            fields[0].transpose(1, 0, 2).reshape(comp * blocks, cells),
            own_weight[0],
            send_weight[0, 0],
            left_weight[0, 0],
        )
        remapped, totals = pl.pallas_call(
            finish,
            out_shape=(
                jax.ShapeDtypeStruct((comp * blocks, cells), F32),
                jax.ShapeDtypeStruct((comp,), F32),
            ),
            in_specs=[vmem, vmem],
            out_specs=(hbm, hbm),
        )(
            pltpu.with_memory_space_constraint(remapped, pltpu.VMEM),
            pltpu.with_memory_space_constraint(totals, pltpu.VMEM),
        )
        remapped = remapped.reshape(comp, blocks, cells).transpose(1, 0, 2)
        return remapped[None], totals

    in_specs = (
        P("level", "dev", None, None),
        P("level", "dev"),
        P("level", "dev", None, None),
        P("level", "dev", None, None),
        P("level", "dev", None, None),
        P("level", "dev", None),
        P("level", "dev", None, None, None, None),
        P("level", "dev", None, None),
        P("level", "dev", None, None),
        P("level", "dev", None),
        P("level", "dev", None, None, None, None),
    )
    out_specs = (P("level", "dev", None, None), P())
    return jax.shard_map(body, mesh=mesh, in_specs=in_specs, out_specs=out_specs, check_vma=False)
```

time: 12.3 us -> 11.6 us (0.943)
  Pallas kernels: 11.5 us -> 10.8 us
    pallas_call x1, Pallas kernels: 10.8 us -> 10.2 us  [body(): pl.pallas_call(functools.partial(kernel, nd, nl, direct), out_shape=(pltp...]
where the time goes in v2:
time: 11.6 us; the launch traced here: 11.5 us
  Pallas kernels  10.8 us (93%)
  between operations  0.64 us (6%)
    pallas_call x1, Pallas kernels, body(): pl.pallas_call(functools.partial(kernel, nd, nl, direct), out_shape=(pltp...  10.2 us
    pallas_call x1, Pallas kernels, body(): pl.pallas_call(finish, out_shape=(jax.ShapeDtypeStruct((comp * blocks, ce...  0.64 us

profile of v2, /device:TPU:0, one launch (start us, length us, event | category | flops | bytes accessed | tf_op | source)
XLA Modules:
  0.0 11.5 jit_solution(5986653057750180552)
XLA Ops:
  0.6 10.2 %shard_map.122 = (f32[192,128]{1,0:T(8,128)S(1)}, f32[12]{0:T(128)S(1)}) custom-call(s32[1,16]{1,0:T(1,128)} %own_src_hbm.1, s32[2,8]{1,0:T(2,128)} %bitcast.31, s32[2,8]{1,0:T(2,128)} %bitcast.32, s32[1,8]{1,0:T(1,128)} %bitcast.35, s32[2,4]{1,0:T(2,128)} %bitcast.33, s32[2,4]{1,0:T(2,128)} %bitcast.34, s32[1,4]{1,0:T(1,128)} %bitcast.36, ...), custom_call_target="tpu_custom_call" | custom-call | tf_op jit(solution)/shard_map/pallas_call | solution.py:280
  10.8 0.6 %shard_map.123 = (f32[192,128]{1,0:T(8,128)}, f32[12]{0:T(128)}) custom-call(f32[192,128]{1,0:T(8,128)S(1)} %get-tuple-element.6.remapped_vmem, f32[12]{0:T(128)S(1)} %get-tuple-element.7.totals_vmem), custom_call_target="tpu_custom_call" | custom-call | tf_op jit(solution)/shard_map/pallas_call | solution.py:324

commit v3 on v2

--- a/solution.py
+++ b/solution.py
@@ -10,7 +10,6 @@
 MESH = pl.DeviceIdType.MESH
 F32 = jnp.float32
 BF16 = jnp.bfloat16
-CHUNKS = 1
 
 
 def tree(terms):
@@ -64,7 +63,7 @@
     comp = fields.shape[0] // blocks
     cap = send_w.shape[1]
     lcap = left_w.shape[1]
-    per = blocks // CHUNKS
+    early = nd // 2
 
     barrier = pltpu.get_barrier_semaphore()
     left_peers = [lax.rem(lvl + r, nl) for r in range(1, nl)]
@@ -79,7 +78,7 @@
     offsets = [
         (l, r)
         for l in (*range(1, nl), 0)
-        for r in (1, 2, 0, *range(3, nd))
+        for r in (*reversed(range(min(3, nd))), *range(3, nd))
         if (l or r) and (direct or not (l and r))
     ]
 
@@ -105,13 +104,9 @@
             )
         ]
         n = len(small)
-        owns = [
-            load(own_hbm.at[i * per : (i + 1) * per], own_w.at[i * per : (i + 1) * per], n + 2 + i)
-            for i in range(CHUNKS)
-        ]
-
+        owns = load(own_hbm, own_w, n + 3)
         for i, p in enumerate(send_peers):
-            load(send_hbm.at[p], send_w.at[i], n + 1)
+            load(send_hbm.at[p], send_w.at[i], n + 1 if i < early else n + 2)
         for i, p in enumerate(left_peers):
             load(left_hbm.at[p], left_w.at[i], n)
 
@@ -131,24 +126,21 @@
 
         line = lax.broadcasted_iota(jnp.int32, (rows, cells), 0)
 
-        held = []
-
-        def messages(buf, slots, slot_block, slot_target, slot_count, weights, peers):
-            keys = [(i, c, p) for i, p in enumerate(peers) for c in range(slots)]
+        send_slots = [(i, c, p) for i, p in enumerate(send_peers) for c in range(cap)]
+        left_slots = [(i, c, p) for i, p in enumerate(left_peers) for c in range(lcap)]
+
+        def gather(slots, slot_block, slot_count, weights):
             pairs = []
-            for i, c, p in keys:
+            for i, c, p in slots:
                 block = donors[slot_block[c, p]]
                 block = jnp.where(c < slot_count[0, p], block, jnp.zeros_like(block))
                 pairs.append((block, weights[i, c]))
-            terms = products(pairs)
-            held.append((buf, slot_target, keys, terms))
-            return terms
-
-        def fill():
-            for buf, slot_target, keys, terms in held:
-                for (i, c, p), term in zip(keys, terms):
-                    filled = jnp.where(line < comp, term, slot_target[c, p].astype(F32))
-                    buf[i, c * rows : (c + 1) * rows, :] = filled.astype(BF16)
+            return pairs
+
+        def fill(buf, slots, slot_target, terms):
+            for (i, c, p), term in zip(slots, terms):
+                filled = jnp.where(line < comp, term, slot_target[c, p].astype(F32))
+                buf[i, c * rows : (c + 1) * rows, :] = filled.astype(BF16)
 
         small[0].wait()
         for b in range(blocks):
@@ -157,17 +149,24 @@
             donors[b] = block.astype(BF16)
         for copy in small[1:]:
             copy.wait()
-        sent = []
-        acc = []
-        for i in range(CHUNKS):
-            owns[i].wait()
-            acc += products([(donors[own_src[0, b]], own_w[b]) for b in range(i * per, (i + 1) * per)])
-
-        settle(send_w, load_sem.at[n + 1])
+        owns.wait()
+        settle(send_w.at[:early], load_sem.at[n + 1])
+        cut = early * cap
+        terms = products(
+            [(donors[own_src[0, b]], own_w[b]) for b in range(blocks)]
+            + gather(send_slots[:cut], send_block, send_count, send_w)
+        )
+        acc, sent = terms[:blocks], terms[blocks:]
+        part = tree(terms)
+        settle(send_w.at[early:], load_sem.at[n + 2])
         settle(left_w, load_sem.at[n])
-        sent += messages(sbuf, cap, send_block, send_target, send_count, send_w, send_peers)
-        sent += messages(lsbuf, lcap, left_block, left_target, left_count, left_w, left_peers)
-        part = tree(sent + acc)
+        terms = products(
+            gather(send_slots[cut:], send_block, send_count, send_w)
+            + gather(left_slots, left_block, left_count, left_w)
+        )
+        sent += terms
+        part += tree(terms)
+
         sums = jnp.sum(part, axis=1, keepdims=True)
         same = line == lax.broadcasted_iota(jnp.int32, (rows, cells), 1)
         row = jnp.sum(jnp.where(same, sums, 0.0), axis=0, keepdims=True)
@@ -191,7 +190,8 @@
         else:
             for r in range(1, nd):
                 send(tbuf.at[0], trecv.at[r - 1], 3, peer_of(0, r))
-        fill()
+        fill(sbuf, send_slots, send_target, sent[: len(send_slots)])
+        fill(lsbuf, left_slots, left_target, sent[len(send_slots) :])
         for r in range(1, nl):
             send(lsbuf.at[r - 1], lrbuf.at[r - 1], 1, peer_of(r, 0))
         for r in range(1, nd):
@@ -228,12 +228,12 @@
             settle(trecv, send_sem.at[3])
 
     pl.run_scoped(
-        run, pltpu.SemaphoreType.DMA((10 + CHUNKS,)), pltpu.SemaphoreType.DMA((recv_sem.shape[0],))
+        run, pltpu.SemaphoreType.DMA((12,)), pltpu.SemaphoreType.DMA((recv_sem.shape[0],))
     )
     settle(urecv, recv_sem.at[0])
     mine = tbuf[0 if direct else 1]
     total = tree([mine] + [urecv[i] for i in range(urecv.shape[0])])
-    tot_ref[...] = (total / (cells * blocks))[0, :comp]
+    tot_ref[...] = (total * (1.0 / (cells * blocks)))[0, :comp]
 
 
 def finish(remapped_vmem, totals_vmem, remapped_hbm, totals_hbm):

time: 11.6 us -> 11.6 us (level)
  no operation moved by 1% of the time
where the time goes in v3:
time: 11.6 us; the launch traced here: 11.5 us
  Pallas kernels  10.8 us (93%)
  between operations  0.64 us (6%)
    pallas_call x1, Pallas kernels, body(): pl.pallas_call(functools.partial(kernel, nd, nl, direct), out_shape=(pltp...  10.2 us
    pallas_call x1, Pallas kernels, body(): pl.pallas_call(finish, out_shape=(jax.ShapeDtypeStruct((comp * blocks, ce...  0.64 us

profile of v3, /device:TPU:0, one launch (start us, length us, event | category | flops | bytes accessed | tf_op | source)
XLA Modules:
  0.0 11.5 jit_solution(12578361829686324777)
XLA Ops:
  0.6 10.2 %shard_map.122 = (f32[192,128]{1,0:T(8,128)S(1)}, f32[12]{0:T(128)S(1)}) custom-call(s32[1,16]{1,0:T(1,128)} %own_src_hbm.1, s32[2,8]{1,0:T(2,128)} %bitcast.31, s32[2,8]{1,0:T(2,128)} %bitcast.32, s32[1,8]{1,0:T(1,128)} %bitcast.35, s32[2,4]{1,0:T(2,128)} %bitcast.33, s32[2,4]{1,0:T(2,128)} %bitcast.34, s32[1,4]{1,0:T(1,128)} %bitcast.36, ...), custom_call_target="tpu_custom_call" | custom-call | tf_op jit(solution)/shard_map/pallas_call | solution.py:280
  10.8 0.6 %shard_map.123 = (f32[192,128]{1,0:T(8,128)}, f32[12]{0:T(128)}) custom-call(f32[192,128]{1,0:T(8,128)S(1)} %get-tuple-element.6.remapped_vmem, f32[12]{0:T(128)S(1)} %get-tuple-element.7.totals_vmem), custom_call_target="tpu_custom_call" | custom-call | tf_op jit(solution)/shard_map/pallas_call | solution.py:324

commit v4 on v3

--- a/solution.py
+++ b/solution.py
@@ -50,8 +50,6 @@
     left_w,
     sbuf,
     rbuf,
-    lsbuf,
-    lrbuf,
     tbuf,
     trecv,
     urecv,
@@ -64,6 +62,7 @@
     cap = send_w.shape[1]
     lcap = left_w.shape[1]
     early = nd // 2
+    base = (nd - 1) * cap
 
     barrier = pltpu.get_barrier_semaphore()
     left_peers = [lax.rem(lvl + r, nl) for r in range(1, nl)]
@@ -137,10 +136,10 @@
                 pairs.append((block, weights[i, c]))
             return pairs
 
-        def fill(buf, slots, slot_target, terms):
-            for (i, c, p), term in zip(slots, terms):
+        def fill(at, slots, slot_target, terms):
+            for k, ((_, c, p), term) in enumerate(zip(slots, terms)):
                 filled = jnp.where(line < comp, term, slot_target[c, p].astype(F32))
-                buf[i, c * rows : (c + 1) * rows, :] = filled.astype(BF16)
+                sbuf[at + k] = filled.astype(BF16)
 
         small[0].wait()
         for b in range(blocks):
@@ -189,15 +188,17 @@
                 send(tbuf.at[0], urecv.at[i], 0, peer_of(l, r))
         else:
             for r in range(1, nd):
-                send(tbuf.at[0], trecv.at[r - 1], 3, peer_of(0, r))
-        fill(sbuf, send_slots, send_target, sent[: len(send_slots)])
-        fill(lsbuf, left_slots, left_target, sent[len(send_slots) :])
+                send(tbuf.at[0], trecv.at[r - 1], 2, peer_of(0, r))
+        fill(0, send_slots, send_target, sent[:base])
+        fill(base, left_slots, left_target, sent[base:])
         for r in range(1, nl):
-            send(lsbuf.at[r - 1], lrbuf.at[r - 1], 1, peer_of(r, 0))
+            part_of = pl.ds(base + (r - 1) * lcap, lcap)
+            send(sbuf.at[part_of], rbuf.at[part_of], 1, peer_of(r, 0))
         for r in range(1, nd):
-            send(sbuf.at[r - 1], rbuf.at[r - 1], 2, peer_of(0, r))
+            part_of = pl.ds((r - 1) * cap, cap)
+            send(sbuf.at[part_of], rbuf.at[part_of], 1, peer_of(0, r))
         if not direct:
-            settle(trecv, recv_sem.at[3])
+            settle(trecv, recv_sem.at[2])
             row = row + jnp.sum(trecv[...], axis=0)
             tbuf[1] = row
             for r in range(1, nl):
@@ -205,27 +206,19 @@
 
         acc = [term[:comp] for term in acc]
 
-        def place(buf, i, slots):
-            for c in range(slots):
-                got = buf[i, c * rows : (c + 1) * rows, :].astype(F32)
-                term = got[:comp]
-                target = jnp.broadcast_to(got[comp : comp + 1], (comp, cells))
-                for b in range(blocks):
-                    acc[b] = acc[b] + jnp.where(target == float(b), term, 0.0)
-
-        settle(rbuf, recv_sem.at[2])
-        for i in range(nd - 1):
-            place(rbuf, i, cap)
-        settle(lrbuf, recv_sem.at[1])
-        for i in range(nl - 1):
-            place(lrbuf, i, lcap)
+        settle(rbuf, recv_sem.at[1])
+        for k in range(rbuf.shape[0]):
+            got = rbuf[k].astype(F32)
+            term = got[:comp]
+            target = jnp.broadcast_to(got[comp : comp + 1], (comp, cells))
+            for b in range(blocks):
+                acc[b] = acc[b] + jnp.where(target == float(b), term, 0.0)
         for b in range(blocks):
             out_ref[pl.ds(b, comp, stride=blocks), :] = acc[b]
-        settle(sbuf, send_sem.at[2])
-        settle(lsbuf, send_sem.at[1])
+        settle(sbuf, send_sem.at[1])
         settle(urecv, send_sem.at[0])
         if not direct:
-            settle(trecv, send_sem.at[3])
+            settle(trecv, send_sem.at[2])
 
     pl.run_scoped(
         run, pltpu.SemaphoreType.DMA((12,)), pltpu.SemaphoreType.DMA((recv_sem.shape[0],))
@@ -298,14 +291,12 @@
                 pltpu.VMEM((blocks, cells, cells), BF16),
                 pltpu.VMEM((nd - 1, cap, cells, cells), BF16),
                 pltpu.VMEM((nl - 1, lcap, cells, cells), BF16),
-                pltpu.VMEM((nd - 1, cap * rows, cells), BF16),
-                pltpu.VMEM((nd - 1, cap * rows, cells), BF16),
-                pltpu.VMEM((nl - 1, lcap * rows, cells), BF16),
-                pltpu.VMEM((nl - 1, lcap * rows, cells), BF16),
+                pltpu.VMEM(((nd - 1) * cap + (nl - 1) * lcap, rows, cells), BF16),
+                pltpu.VMEM(((nd - 1) * cap + (nl - 1) * lcap, rows, cells), BF16),
                 pltpu.VMEM((2, 1, cells), F32),
                 pltpu.VMEM((nd - 1, 1, cells), F32),
                 pltpu.VMEM((last, 1, cells), F32),
-                dma((3 if direct else 4,)),
+                dma((2 if direct else 3,)),
             ],
             compiler_params=pltpu.CompilerParams(collective_id=0, has_side_effects=True),
         )(

time: 11.6 us -> 11.6 us (level)
  no operation moved by 1% of the time
where the time goes in v4:
time: 11.6 us; the launch traced here: 11.5 us
  Pallas kernels  10.8 us (93%)
  between operations  0.64 us (6%)
    pallas_call x1, Pallas kernels, body(): pl.pallas_call(functools.partial(kernel, nd, nl, direct), out_shape=(pltp...  10.2 us
    pallas_call x1, Pallas kernels, body(): pl.pallas_call(finish, out_shape=(jax.ShapeDtypeStruct((comp * blocks, ce...  0.64 us

profile of v4, /device:TPU:0, one launch (start us, length us, event | category | flops | bytes accessed | tf_op | source)
XLA Modules:
  0.0 11.5 jit_solution(4149724482237014101)
XLA Ops:
  0.6 10.2 %shard_map.122 = (f32[192,128]{1,0:T(8,128)S(1)}, f32[12]{0:T(128)S(1)}) custom-call(s32[1,16]{1,0:T(1,128)} %own_src_hbm.1, s32[2,8]{1,0:T(2,128)} %bitcast.31, s32[2,8]{1,0:T(2,128)} %bitcast.32, s32[1,8]{1,0:T(1,128)} %bitcast.35, s32[2,4]{1,0:T(2,128)} %bitcast.33, s32[2,4]{1,0:T(2,128)} %bitcast.34, s32[1,4]{1,0:T(1,128)} %bitcast.36, ...), custom_call_target="tpu_custom_call" | custom-call | tf_op jit(solution)/shard_map/pallas_call | solution.py:273
  10.8 0.6 %shard_map.123 = (f32[192,128]{1,0:T(8,128)}, f32[12]{0:T(128)}) custom-call(f32[192,128]{1,0:T(8,128)S(1)} %get-tuple-element.6.remapped_vmem, f32[12]{0:T(128)S(1)} %get-tuple-element.7.totals_vmem), custom_call_target="tpu_custom_call" | custom-call | tf_op jit(solution)/shard_map/pallas_call | solution.py:315
